TPU v7x, 128 devices: a whole 4x4x4 slice. The times are simulated.
128 devices in a mesh: row: 8 (over x_lo, z), col: 16 (over y, x_hi, core).
Axes of the slice: x: 4 (x_hi: 2, x_lo: 2; x = x_hi * 2 + x_lo), y: 4, z: 4, core: 2. Of those that a mesh axis runs over, the one named last changes fastest.
Arguments:
- q_base: bfloat16 [8192, 8192], P('row', 'col'), may hold values from -600 to 600
- q_down: bfloat16 [64, 8192], P(None, 'col'), may hold values from -1.1953125 to 1.1953125
- q_up: bfloat16 [8192, 64], P('row'), may hold values from -1.1953125 to 1.1953125
- q_magnitude: float32 [8192], P('row'), may hold values from 40 to 200
- k_base: bfloat16 [1024, 8192], P('row', 'col'), may hold values from -600 to 600
- k_down: bfloat16 [64, 8192], P(None, 'col'), may hold values from -1.1953125 to 1.1953125
- k_up: bfloat16 [1024, 64], P('row'), may hold values from -1.1953125 to 1.1953125
- k_magnitude: float32 [1024], P('row'), may hold values from 40 to 200
- v_base: bfloat16 [1024, 8192], P('row', 'col'), may hold values from -600 to 600
- v_down: bfloat16 [64, 8192], P(None, 'col'), may hold values from -1.1953125 to 1.1953125
- v_up: bfloat16 [1024, 64], P('row'), may hold values from -1.1953125 to 1.1953125
- v_magnitude: float32 [1024], P('row'), may hold values from 40 to 200
- o_base: bfloat16 [8192, 8192], P('row', 'col'), may hold values from -600 to 600
- o_down: bfloat16 [64, 8192], P(None, 'col'), may hold values from -1.1953125 to 1.1953125
- o_up: bfloat16 [8192, 64], P('row'), may hold values from -1.1953125 to 1.1953125
- o_magnitude: float32 [8192], P('row'), may hold values from 40 to 200
- gate_base: bfloat16 [29568, 8192], P('row', 'col'), may hold values from -600 to 600
- gate_down: bfloat16 [64, 8192], P(None, 'col'), may hold values from -1.1953125 to 1.1953125
- gate_up: bfloat16 [29568, 64], P('row'), may hold values from -1.1953125 to 1.1953125
- gate_magnitude: float32 [29568], P('row'), may hold values from 40 to 200
- lift_base: bfloat16 [29568, 8192], P('row', 'col'), may hold values from -600 to 600
- lift_down: bfloat16 [64, 8192], P(None, 'col'), may hold values from -1.1953125 to 1.1953125
- lift_up: bfloat16 [29568, 64], P('row'), may hold values from -1.1953125 to 1.1953125
- lift_magnitude: float32 [29568], P('row'), may hold values from 40 to 200
Outputs:
- q_merged: bfloat16 [8192, 8192], P(('row', 'col'))
- k_merged: bfloat16 [1024, 8192], P(('row', 'col'))
- v_merged: bfloat16 [1024, 8192], P(('row', 'col'))
- o_merged: bfloat16 [8192, 8192], P(None, ('col', 'row'))
- gate_merged: bfloat16 [29568, 8192], P(('row', 'col'))
- lift_merged: bfloat16 [29568, 8192], P(('row', 'col'))
All inputs are finite; a program needn't handle non-finite values.
Results may differ from a plain program's by a relative error of at most 0.001.
Values may be sent and summed in bfloat16 or wider, within the bound.
A program may use at most 128 MiB of HBM per device.

v0:
```python
import jax
import jax.numpy as jnp
from jax import lax
from jax.sharding import Mesh
from jax.sharding import PartitionSpec as P

COL = ("col_0", "col_1", "col_2")
ROW_COL = ("row", "col_0", "col_1", "col_2")
COL_ROW = ("col_0", "col_1", "col_2", "row")
eps = 1e-06


def over_axes(value, axes):
    for axis in axes:
        value = lax.psum(value, axis)
    return value


def tile_merge(base, down, up, magnitude):
    direction = base.astype(jnp.float32) + jnp.dot(up, down, preferred_element_type=jnp.float32)
    partial_sum = jnp.sum(direction * direction, axis=1)
    total = over_axes(partial_sum, COL)
    factor = magnitude * lax.rsqrt(total + eps)
    return (direction * factor[:, None]).astype(jnp.bfloat16)


def row_split(base, down, up, magnitude):
    merged = tile_merge(base, down, up, magnitude)
    return lax.all_to_all(merged, COL, split_axis=0, concat_axis=1, tiled=True)


def on_device(
    q_base,
    q_down,
    q_up,
    q_magnitude,
    k_base,
    k_down,
    k_up,
    k_magnitude,
    v_base,
    v_down,
    v_up,
    v_magnitude,
    o_base,
    o_down,
    o_up,
    o_magnitude,
    gate_base,
    gate_down,
    gate_up,
    gate_magnitude,
    lift_base,
    lift_down,
    lift_up,
    lift_magnitude,
):
    q_merged = row_split(q_base, q_down, q_up, q_magnitude)
    k_merged = row_split(k_base, k_down, k_up, k_magnitude)
    v_merged = row_split(v_base, v_down, v_up, v_magnitude)
    o_tile = tile_merge(o_base, o_down, o_up, o_magnitude)
    o_merged = lax.all_to_all(o_tile, "row", split_axis=1, concat_axis=0, tiled=True)
    gate_merged = row_split(gate_base, gate_down, gate_up, gate_magnitude)
    lift_merged = row_split(lift_base, lift_down, lift_up, lift_magnitude)
    return (q_merged, k_merged, v_merged, o_merged, gate_merged, lift_merged)


def solution(mesh):
    finer = Mesh(
        mesh.devices.reshape(mesh.shape["row"], 4, 2, 2), ("row", "col_0", "col_1", "col_2")
    )
    placed = (
        P("row", COL),
        P(None, COL),
        P("row", None),
        P("row"),
        P("row", COL),
        P(None, COL),
        P("row", None),
        P("row"),
        P("row", COL),
        P(None, COL),
        P("row", None),
        P("row"),
        P("row", COL),
        P(None, COL),
        P("row", None),
        P("row"),
        P("row", COL),
        P(None, COL),
        P("row", None),
        P("row"),
        P("row", COL),
        P(None, COL),
        P("row", None),
        P("row"),
    )
    return jax.shard_map(
        on_device,
        mesh=finer,
        in_specs=placed,
        out_specs=(
            P(ROW_COL, None),
            P(ROW_COL, None),
            P(ROW_COL, None),
            P(None, COL_ROW),
            P(ROW_COL, None),
            P(ROW_COL, None),
        ),
        check_vma=False,
    )
```

profile of v0, /device:TPU:1, one launch (start us, length us, event | category | flops | bytes accessed | tf_op | source)
XLA Modules:
  0.0 232.9 jit_solution(16911114155286947436)
XLA Ops:
  0.6 0.0 copy-start
  0.6 0.0 copy-start.5
  0.7 0.0 copy-start.8
  0.7 1.5 copy.39
  2.2 0.0 copy-start.2
  2.2 0.0 copy-start.6
  2.2 1.4 multiply_reduce_fusion.5
  3.6 1.3 multiply_reduce_fusion.4
  4.9 2.7 %multiply_reduce_fusion.2 = (f32[1024]{0:T(1024)S(1)}, f32[1024,512]{0,1:T(8,128)}) fusion(bf16[1024,64]{0,1:T(8,128)(2,1)} %param.38, bf16[64,512]{1,0:T(8,128)(2,1)} %param.37, bf16[1024,512]{0,1:T(8,128)(2,1)S(1)} %copy.39), kind=kOutput, calls=%fused_computation.7 | convolution fusion | flops 69204992 | bytes 3346432 | tf_op jit(solution)/shard_map/dot_general | solution.py:20
  7.6 0.0 copy-done.5
  7.6 0.0 copy-done.8
  7.6 1.8 multiply_reduce_fusion.3
  9.4 0.0 copy-done
  9.4 0.0 copy-done.2
  9.4 0.0 copy-done.6
  9.4 0.0 copy-start.3
  9.4 0.0 copy-start.4
  9.5 0.0 copy-start.7
  9.5 4.3 %multiply_reduce_fusion.1 = (f32[3696]{0:T(1024)S(1)}, f32[3696,512]{1,0:T(8,128)}) fusion(bf16[3696,64]{0,1:T(8,128)(2,1)S(1)} %copy-done, bf16[64,512]{1,0:T(8,128)(2,1)S(1)} %copy-done.6, bf16[3696,512]{1,0:T(8,128)(2,1)S(1)} %copy-done.2), kind=kOutput, calls=%fused_computation.4 | convolution fusion | flops 249786768 | bytes 11907520 | tf_op jit(solution)/shard_map/dot_general | solution.py:20
  13.8 0.0 copy-done.3
  13.8 0.0 copy-done.4
  13.8 0.0 copy-done.7
  13.8 0.0 copy-start.14
  13.8 0.0 copy-start.11
  13.8 0.0 copy-start.12
  13.8 4.4 %multiply_reduce_fusion = (f32[3696]{0:T(1024)S(1)}, f32[3696,512]{1,0:T(8,128)}) fusion(bf16[3696,64]{0,1:T(8,128)(2,1)S(1)} %copy-done.4, bf16[64,512]{1,0:T(8,128)(2,1)S(1)} %copy-done.7, bf16[3696,512]{1,0:T(8,128)(2,1)S(1)} %copy-done.3), kind=kOutput, calls=%fused_computation.1 | convolution fusion | flops 249786768 | bytes 11907520 | tf_op jit(solution)/shard_map/dot_general | solution.py:20
  18.2 14.8 %all-reduce = (f32[1024]{0:T(1024)S(1)}, f32[128]{0:T(128)S(1)}, f32[128]{0:T(128)S(1)}, f32[1024]{0:T(1024)S(1)}, f32[3696]{0:T(1024)S(1)}, /*index=5*/f32[3696]{0:T(1024)S(1)}) all-reduce(f32[1024]{0:T(1024)S(1)} %get-tuple-element.24, ...), channel_id=1, replica_groups=mesh['row'=8,'col_0'=4,'col_1'=2,'col_2'=2] {'col_0'}, use_global_device_ids=true, to_apply=%region_1.0 | all-reduce | flops 9696 | bytes 77568 | tf_op jit(solution)/shard_map/psum | solution.py:15
  33.0 9.6 %all-reduce.2 = (f32[1024]{0:T(1024)S(1)}, f32[128]{0:T(128)S(1)}, f32[128]{0:T(128)S(1)}, f32[1024]{0:T(1024)S(1)}, f32[3696]{0:T(1024)S(1)}, /*index=5*/f32[3696]{0:T(1024)S(1)}) all-reduce(f32[1024]{0:T(1024)S(1)} %get-tuple-element.6, ...), channel_id=1, replica_groups=mesh['row'=8,'col_0'=4,'col_1'=2,'col_2'=2] {'col_1'}, use_global_device_ids=true, to_apply=%region_2.0 | all-reduce | flops 9696 | bytes 77568 | tf_op jit(solution)/shard_map/psum | solution.py:15
  42.7 9.8 %all-reduce.1 = (f32[1024]{0:T(1024)S(1)}, f32[128]{0:T(128)S(1)}, f32[128]{0:T(128)S(1)}, f32[1024]{0:T(1024)S(1)}, f32[3696]{0:T(1024)S(1)}, /*index=5*/f32[3696]{0:T(1024)S(1)}) all-reduce(f32[1024]{0:T(1024)S(1)} %get-tuple-element.18, ...), channel_id=1, replica_groups=mesh['row'=8,'col_0'=4,'col_1'=2,'col_2'=2] {'col_2'}, use_global_device_ids=true, to_apply=%region_3.0 | all-reduce | flops 9696 | bytes 77568 | tf_op jit(solution)/shard_map/psum | solution.py:15
  52.5 0.0 copy-done.13
  52.5 0.7 fusion.1
  53.2 3.5 %all-to-all-start.2 = ((bf16[16,8,512]{2,1,0:T(8,128)(2,1)}), bf16[16,8,512]{2,1,0:T(8,128)(2,1)S(1)}, u32[]{:S(2)}, u32[]{:S(2)}) async-start(bf16[16,8,512]{2,1,0:T(8,128)(2,1)} %fusion.1), calls=%async_computation.2 | async-start | bytes 262144 | tf_op jit(solution)/shard_map/all_to_all | solution.py:29
  56.7 0.0 copy-done.14
  56.7 0.7 fusion
  57.5 0.0 copy-done.11
  57.5 0.0 copy-done.12
  57.5 6.9 %all-to-all-done.2 = bf16[16,8,512]{2,1,0:T(8,128)(2,1)S(1)} async-done(((bf16[16,8,512]{2,1,0:T(8,128)(2,1)}), bf16[16,8,512]{2,1,0:T(8,128)(2,1)S(1)}, u32[]{:S(2)}, u32[]{:S(2)}) %all-to-all-start.2) | async-done | bytes 131104 | tf_op jit(solution)/shard_map/all_to_all | solution.py:29
  64.4 4.0 %all-to-all-start.1 = ((bf16[16,8,512]{2,1,0:T(8,128)(2,1)}), bf16[16,8,512]{2,1,0:T(8,128)(2,1)S(1)}, u32[]{:S(2)}, u32[]{:S(2)}) async-start(bf16[16,8,512]{2,1,0:T(8,128)(2,1)} %fusion), calls=%async_computation.1 | async-start | bytes 262144 | tf_op jit(solution)/shard_map/all_to_all | solution.py:29
  68.4 2.8 %multiply_convert_fusion.2 = bf16[1024,512]{0,1:T(8,128)(2,1)} fusion(f32[1024,512]{0,1:T(8,128)} %get-tuple-element.31, f32[1024]{0:T(1024)S(1)} %get-tuple-element.38), kind=kLoop, calls=%fused_computation.6 | loop fusion | flops 1048576 | bytes 3149824 | tf_op jit(solution)/shard_map/convert_element_type | solution.py:24
  71.2 4.9 %all-to-all-done.1 = bf16[16,8,512]{2,1,0:T(8,128)(2,1)S(1)} async-done(((bf16[16,8,512]{2,1,0:T(8,128)(2,1)}), bf16[16,8,512]{2,1,0:T(8,128)(2,1)S(1)}, u32[]{:S(2)}, u32[]{:S(2)}) %all-to-all-start.1) | async-done | bytes 131104 | tf_op jit(solution)/shard_map/all_to_all | solution.py:29
  76.1 5.2 %all-to-all-start.3 = ((bf16[1024,8,64]{0,2,1:T(8,128)(2,1)}), bf16[1024,8,64]{0,2,1:T(8,128)(2,1)}, u32[]{:S(2)}, u32[]{:S(2)}) async-start(bf16[1024,8,64]{0,2,1:T(8,128)(2,1)} %bitcast.41), calls=%async_computation.3 | async-start | bytes 2097152 | tf_op jit(solution)/shard_map/all_to_all | solution.py:62
  81.3 1.2 multiply_convert_fusion.3
  82.5 14.0 %all-to-all-done.3 = bf16[1024,8,64]{0,2,1:T(8,128)(2,1)} async-done(((bf16[1024,8,64]{0,2,1:T(8,128)(2,1)}), bf16[1024,8,64]{0,2,1:T(8,128)(2,1)}, u32[]{:S(2)}, u32[]{:S(2)}) %all-to-all-start.3) | async-done | bytes 1048608 | tf_op jit(solution)/shard_map/all_to_all | solution.py:62
  96.5 4.1 %all-to-all-start = ((bf16[16,64,512]{2,1,0:T(8,128)(2,1)}), bf16[16,64,512]{2,1,0:T(8,128)(2,1)S(1)}, u32[]{:S(2)}, u32[]{:S(2)}) async-start(bf16[16,64,512]{2,1,0:T(8,128)(2,1)} %bitcast.42), calls=%async_computation | async-start | bytes 2097152 | tf_op jit(solution)/shard_map/all_to_all | solution.py:29
  100.7 5.3 %multiply_convert_fusion = bf16[3696,512]{1,0:T(8,128)(2,1)} fusion(f32[3696,512]{1,0:T(8,128)} %get-tuple-element.35, f32[3696]{0:T(1024)S(1)} %get-tuple-element.36), kind=kLoop, calls=%fused_computation | loop fusion | flops 3784704 | bytes 11368896 | tf_op jit(solution)/shard_map/convert_element_type | solution.py:24
  106.0 4.0 %all_to_all.104 = bf16[16,231,512]{2,1,0:T(8,128)(2,1)} reshape(bf16[3696,512]{1,0:T(8,128)(2,1)} %multiply_convert_fusion) | data formatting | bytes 7569408 | tf_op jit(solution)/shard_map/all_to_all | solution.py:29
  109.9 7.9 %all-to-all-done = bf16[16,64,512]{2,1,0:T(8,128)(2,1)S(1)} async-done(((bf16[16,64,512]{2,1,0:T(8,128)(2,1)}), bf16[16,64,512]{2,1,0:T(8,128)(2,1)S(1)}, u32[]{:S(2)}, u32[]{:S(2)}) %all-to-all-start) | async-done | bytes 1048608 | tf_op jit(solution)/shard_map/all_to_all | solution.py:29
  117.9 5.2 %all-to-all-start.5 = ((bf16[16,231,512]{2,1,0:T(8,128)(2,1)}), bf16[16,231,512]{2,1,0:T(8,128)(2,1)}, u32[]{:S(2)}, u32[]{:S(2)}) async-start(bf16[16,231,512]{2,1,0:T(8,128)(2,1)} %all_to_all.104), calls=%async_computation.5 | async-start | bytes 7602176 | tf_op jit(solution)/shard_map/all_to_all | solution.py:29
  123.1 5.3 %multiply_convert_fusion.1 = bf16[3696,512]{1,0:T(8,128)(2,1)} fusion(f32[3696,512]{1,0:T(8,128)} %get-tuple-element.33, f32[3696]{0:T(1024)S(1)} %get-tuple-element.37), kind=kLoop, calls=%fused_computation.3 | loop fusion | flops 3784704 | bytes 11368896 | tf_op jit(solution)/shard_map/convert_element_type | solution.py:24
  128.4 4.0 %all_to_all.100 = bf16[16,231,512]{2,1,0:T(8,128)(2,1)} reshape(bf16[3696,512]{1,0:T(8,128)(2,1)} %multiply_convert_fusion.1) | data formatting | bytes 7569408 | tf_op jit(solution)/shard_map/all_to_all | solution.py:29
  132.4 37.6 %all-to-all-done.5 = bf16[16,231,512]{2,1,0:T(8,128)(2,1)} async-done(((bf16[16,231,512]{2,1,0:T(8,128)(2,1)}), bf16[16,231,512]{2,1,0:T(8,128)(2,1)}, u32[]{:S(2)}, u32[]{:S(2)}) %all-to-all-start.5) | async-done | bytes 3784736 | tf_op jit(solution)/shard_map/all_to_all | solution.py:29
  169.9 5.3 %all-to-all-start.4 = ((bf16[16,231,512]{2,1,0:T(8,128)(2,1)}), bf16[16,231,512]{2,1,0:T(8,128)(2,1)}, u32[]{:S(2)}, u32[]{:S(2)}) async-start(bf16[16,231,512]{2,1,0:T(8,128)(2,1)} %all_to_all.100), calls=%async_computation.4 | async-start | bytes 7602176 | tf_op jit(solution)/shard_map/all_to_all | solution.py:29
  175.2 2.3 copy.44
  177.5 1.1 copy.43
  178.5 3.4 %copy.42 = bf16[231,16,512]{2,1,0:T(8,128)(2,1)S(1)} copy(bf16[231,16,512]{2,0,1:T(8,128)(2,1)} %bitcast.11) | data formatting | bytes 7569408 | tf_op jit(solution)/shard_map/all_to_all | solution.py:29
  181.9 0.4 pad.1
  182.3 5.8 %copy.46 = bf16[29,8,16,512]{3,1,2,0:T(8,128)(2,1)} copy(bf16[29,8,16,512]{3,2,1,0:T(8,128)(2,1)S(1)} %bitcast.39) | data formatting | bytes 7602176
  188.1 33.9 %all-to-all-done.4 = bf16[16,231,512]{2,1,0:T(8,128)(2,1)} async-done(((bf16[16,231,512]{2,1,0:T(8,128)(2,1)}), bf16[16,231,512]{2,1,0:T(8,128)(2,1)}, u32[]{:S(2)}, u32[]{:S(2)}) %all-to-all-start.4) | async-done | bytes 3784736 | tf_op jit(solution)/shard_map/all_to_all | solution.py:29
  222.0 3.4 %copy.41 = bf16[231,16,512]{2,1,0:T(8,128)(2,1)S(1)} copy(bf16[231,16,512]{2,0,1:T(8,128)(2,1)} %bitcast.10) | data formatting | bytes 7569408 | tf_op jit(solution)/shard_map/all_to_all | solution.py:29
  225.4 0.4 pad
  225.8 0.0 copy-start.1
  225.8 5.8 %copy.45 = bf16[29,8,16,512]{3,1,2,0:T(8,128)(2,1)} copy(bf16[29,8,16,512]{3,2,1,0:T(8,128)(2,1)S(1)} %bitcast.38) | data formatting | bytes 7602176
  231.5 0.7 copy.49
  232.2 0.7 copy.50
  (10 shorter events, 0.0 us)
Async XLA Ops:
  0.6 8.8 %copy-start = (bf16[3696,64]{0,1:T(8,128)(2,1)S(1)}, bf16[3696,64]{0,1:T(8,128)(2,1)}, u32[]{:S(2)}) copy-start(bf16[3696,64]{0,1:T(8,128)(2,1)} %param.42) | copy-start | bytes 1419268
  0.6 7.0 %copy-start.5 = (bf16[1024,64]{0,1:T(8,128)(2,1)S(1)}, bf16[1024,64]{0,1:T(8,128)(2,1)}, u32[]{:S(2)}) copy-start(bf16[1024,64]{0,1:T(8,128)(2,1)} %param.26) | copy-start | bytes 393220
  0.7 7.0 %copy-start.8 = (bf16[64,512]{1,0:T(8,128)(2,1)S(1)}, bf16[64,512]{1,0:T(8,128)(2,1)}, u32[]{:S(2)}) copy-start(bf16[64,512]{1,0:T(8,128)(2,1)} %param.25) | copy-start | bytes 196612
  2.2 7.2 %copy-start.2 = (bf16[3696,512]{1,0:T(8,128)(2,1)S(1)}, bf16[3696,512]{1,0:T(8,128)(2,1)}, u32[]{:S(2)}) copy-start(bf16[3696,512]{1,0:T(8,128)(2,1)} %param.40) | copy-start | bytes 11354116
  2.2 7.2 %copy-start.6 = (bf16[64,512]{1,0:T(8,128)(2,1)S(1)}, bf16[64,512]{1,0:T(8,128)(2,1)}, u32[]{:S(2)}) copy-start(bf16[64,512]{1,0:T(8,128)(2,1)} %param.41) | copy-start | bytes 196612
  9.4 4.3 %copy-start.3 = (bf16[3696,512]{1,0:T(8,128)(2,1)S(1)}, bf16[3696,512]{1,0:T(8,128)(2,1)}, u32[]{:S(2)}) copy-start(bf16[3696,512]{1,0:T(8,128)(2,1)} %param.44) | copy-start | bytes 11354116
  9.4 4.3 %copy-start.4 = (bf16[3696,64]{0,1:T(8,128)(2,1)S(1)}, bf16[3696,64]{0,1:T(8,128)(2,1)}, u32[]{:S(2)}) copy-start(bf16[3696,64]{0,1:T(8,128)(2,1)} %param.46) | copy-start | bytes 1419268
  9.5 4.3 %copy-start.7 = (bf16[64,512]{1,0:T(8,128)(2,1)S(1)}, bf16[64,512]{1,0:T(8,128)(2,1)}, u32[]{:S(2)}) copy-start(bf16[64,512]{1,0:T(8,128)(2,1)} %param.45) | copy-start | bytes 196612
  13.8 38.7 %copy-start.13 = (f32[128]{0:T(128)S(1)}, f32[128]{0:T(128)}, u32[]{:S(2)}) copy-start(f32[128]{0:T(128)} %param.35) | copy-start | bytes 1540
  13.8 42.9 %copy-start.14 = (f32[128]{0:T(128)S(1)}, f32[128]{0:T(128)}, u32[]{:S(2)}) copy-start(f32[128]{0:T(128)} %param.31) | copy-start | bytes 1540
  13.8 43.7 %copy-start.11 = (f32[1024]{0:T(1024)S(1)}, f32[1024]{0:T(1024)}, u32[]{:S(2)}) copy-start(f32[1024]{0:T(1024)} %param.39) | copy-start | bytes 12292
  13.8 43.7 %copy-start.12 = (f32[1024]{0:T(1024)S(1)}, f32[1024]{0:T(1024)}, u32[]{:S(2)}) copy-start(f32[1024]{0:T(1024)} %param.27) | copy-start | bytes 12292
  18.2 63.1 %copy-start.9 = (f32[3696]{0:T(1024)S(1)}, f32[3696]{0:T(1024)}, u32[]{:S(2)}) copy-start(f32[3696]{0:T(1024)} %param.47) | copy-start | bytes 44356
  18.2 63.1 %copy-start.10 = (f32[3696]{0:T(1024)S(1)}, f32[3696]{0:T(1024)}, u32[]{:S(2)}) copy-start(f32[3696]{0:T(1024)} %param.43) | copy-start | bytes 44356
  53.2 11.2 %all-to-all-start.2 = ((bf16[16,8,512]{2,1,0:T(8,128)(2,1)}), bf16[16,8,512]{2,1,0:T(8,128)(2,1)S(1)}, u32[]{:S(2)}, u32[]{:S(2)}) async-start(bf16[16,8,512]{2,1,0:T(8,128)(2,1)} %fusion.1), calls=%async_computation.2 | async-start | bytes 262144 | tf_op jit(solution)/shard_map/all_to_all | solution.py:29
  64.4 11.7 %all-to-all-start.1 = ((bf16[16,8,512]{2,1,0:T(8,128)(2,1)}), bf16[16,8,512]{2,1,0:T(8,128)(2,1)S(1)}, u32[]{:S(2)}, u32[]{:S(2)}) async-start(bf16[16,8,512]{2,1,0:T(8,128)(2,1)} %fusion), calls=%async_computation.1 | async-start | bytes 262144 | tf_op jit(solution)/shard_map/all_to_all | solution.py:29
  76.1 20.4 %all-to-all-start.3 = ((bf16[1024,8,64]{0,2,1:T(8,128)(2,1)}), bf16[1024,8,64]{0,2,1:T(8,128)(2,1)}, u32[]{:S(2)}, u32[]{:S(2)}) async-start(bf16[1024,8,64]{0,2,1:T(8,128)(2,1)} %bitcast.41), calls=%async_computation.3 | async-start | bytes 2097152 | tf_op jit(solution)/shard_map/all_to_all | solution.py:62
  96.5 21.3 %all-to-all-start = ((bf16[16,64,512]{2,1,0:T(8,128)(2,1)}), bf16[16,64,512]{2,1,0:T(8,128)(2,1)S(1)}, u32[]{:S(2)}, u32[]{:S(2)}) async-start(bf16[16,64,512]{2,1,0:T(8,128)(2,1)} %bitcast.42), calls=%async_computation | async-start | bytes 2097152 | tf_op jit(solution)/shard_map/all_to_all | solution.py:29
  117.9 52.0 %all-to-all-start.5 = ((bf16[16,231,512]{2,1,0:T(8,128)(2,1)}), bf16[16,231,512]{2,1,0:T(8,128)(2,1)}, u32[]{:S(2)}, u32[]{:S(2)}) async-start(bf16[16,231,512]{2,1,0:T(8,128)(2,1)} %all_to_all.104), calls=%async_computation.5 | async-start | bytes 7602176 | tf_op jit(solution)/shard_map/all_to_all | solution.py:29
  169.9 52.1 %all-to-all-start.4 = ((bf16[16,231,512]{2,1,0:T(8,128)(2,1)}), bf16[16,231,512]{2,1,0:T(8,128)(2,1)}, u32[]{:S(2)}, u32[]{:S(2)}) async-start(bf16[16,231,512]{2,1,0:T(8,128)(2,1)} %all_to_all.100), calls=%async_computation.4 | async-start | bytes 7602176 | tf_op jit(solution)/shard_map/all_to_all | solution.py:29
  225.8 7.1 %copy-start.1 = (bf16[3696,64]{0,1:T(8,128)(2,1)S(1)}, bf16[3696,64]{0,1:T(8,128)(2,1)}, u32[]{:S(2)}) copy-start(bf16[3696,64]{0,1:T(8,128)(2,1)} %param.42) | copy-start | bytes 1419268
where the time goes:
time: 234 us; the launch traced here: 233 us
  waiting for transfers between devices  105 us (45%)
  blocking collectives  34.2 us (15%)
  local copies, waits for them, and re-layouts  33.2 us (14%)
  starting transfers between devices  27.3 us (12%)
  other arithmetic  16.1 us (7%)
  matrix products  15.8 us (7%)
    all_to_all x5, waiting for transfers between devices, row_split(): return lax.all_to_all(merged, COL, split_axis=0, concat_axis=1, tiled=True)  91.2 us
    psum x3, blocking collectives, over_axes(): value = lax.psum(value, axis)  34.2 us
    all_to_all x5, starting transfers between devices, row_split(): return lax.all_to_all(merged, COL, split_axis=0, concat_axis=1, tiled=True)  22.2 us
    dot_general x6, matrix products, tile_merge(): jnp.dot(up, down, preferred_element_type=jnp.float32)  15.8 us
    all_to_all x5, local copies, waits for them, and re-layouts, row_split(): return lax.all_to_all(merged, COL, split_axis=0, concat_axis=1, tiled=True)  15.7 us
    unnamed x37, local copies, waits for them, and re-layouts  15.3 us
    convert_element_type x4, other arithmetic, tile_merge(): return (direction * factor[:, None]).astype(jnp.bfloat16)  14.6 us
    all_to_all x1, waiting for transfers between devices, on_device(): lax.all_to_all(o_tile, 'row', split_axis=1, concat_axis=0, tiled=True)  14 us
  transfers between devices with their start and end apart: 6, of which 6 were waited for; matrix products, arithmetic and copies ran while one was open for 12% of the time, Pallas kernels for 0%

commit v1 on v0

--- a/solution.py
+++ b/solution.py
@@ -12,7 +12,8 @@
 
 def over_axes(value, axes):
     for axis in axes:
-        value = lax.psum(value, axis)
+        part_next = lax.all_gather(value, axis_name=axis)
+        value = jnp.sum(part_next, 0)
     return value
 
 

time: 234 us -> 298 us (1.27)
  blocking collectives: 34.2 us -> 89.8 us
  waiting for transfers between devices: 105 us -> 85.5 us
  between operations: 0.88 us -> 16.5 us
  local copies, waits for them, and re-layouts: 33.2 us -> 40.7 us
  starting transfers between devices: 27.3 us -> 30.5 us
    all_gather x0 -> x12, blocking collectives: none -> 76.1 us  [over_axes(): part_next = lax.all_gather(value, axis_name=axis)]
    psum x3 -> x0, blocking collectives: 34.2 us -> none  [over_axes(): value = lax.psum(value, axis)]
    all_to_all x1, waiting for transfers between devices: 14 us -> 0.01 us  [on_device(): lax.all_to_all(o_tile, 'row', split_axis=1, concat_axis=0, tiled=True)]
    unnamed x0 -> x2, blocking collectives: none -> 13.7 us
    all_to_all x5, waiting for transfers between devices: 91.2 us -> 85.5 us  [row_split(): return lax.all_to_all(merged, COL, split_axis=0, concat_axis=1, tiled=True)]
    unnamed x37 -> x64, local copies, waits for them, and re-layouts: 15.3 us -> 20.4 us
    all_to_all x5, starting transfers between devices: 22.2 us -> 25.4 us  [row_split(): return lax.all_to_all(merged, COL, split_axis=0, concat_axis=1, tiled=True)]
  transfers between devices with their start and end apart: 6 -> 7, of which waited for: 6 -> 4; matrix products, arithmetic and copies ran while one was open for 12% -> 18% of each run, Pallas kernels for 0% -> 0%
where the time goes in v1:
time: 298 us; the launch traced here: 297 us
  blocking collectives  89.8 us (30%)
  waiting for transfers between devices  85.5 us (29%)
  local copies, waits for them, and re-layouts  40.7 us (14%)
  starting transfers between devices  30.5 us (10%)
  matrix products  18 us (6%)
  between operations  16.5 us (6%)
  other arithmetic  15.7 us (5%)
    all_to_all x5, waiting for transfers between devices, row_split(): return lax.all_to_all(merged, COL, split_axis=0, concat_axis=1, tiled=True)  85.5 us
    all_gather x12, blocking collectives, over_axes(): part_next = lax.all_gather(value, axis_name=axis)  76.1 us
    all_to_all x5, starting transfers between devices, row_split(): return lax.all_to_all(merged, COL, split_axis=0, concat_axis=1, tiled=True)  25.4 us
    unnamed x64, local copies, waits for them, and re-layouts  20.4 us
    dot_general x6, matrix products, tile_merge(): jnp.dot(up, down, preferred_element_type=jnp.float32)  18 us
    all_to_all x5, local copies, waits for them, and re-layouts, row_split(): return lax.all_to_all(merged, COL, split_axis=0, concat_axis=1, tiled=True)  15.7 us
    unnamed x2, blocking collectives  13.7 us
    convert_element_type x4, other arithmetic, tile_merge(): return (direction * factor[:, None]).astype(jnp.bfloat16)  13 us
  transfers between devices with their start and end apart: 7, of which 4 were waited for; matrix products, arithmetic and copies ran while one was open for 18% of the time, Pallas kernels for 0%

profile of v1, /device:TPU:1, one launch (start us, length us, event | category | flops | bytes accessed | tf_op | source)
XLA Modules:
  0.0 296.6 jit_solution(1188839877107082963)
XLA Ops:
  7.2 1.3 multiply_reduce_fusion.5
  8.5 8.8 %all-gather.18 = f32[4,1,128]{2,1,0:T(1,128)S(1)} all-gather(f32[1,1,128]{2,1,0:T(1,128)S(1)} %bitcast.58), channel_id=5, replica_groups=mesh['row'=8,'col_0'=4,'col_1'=2,'col_2'=2] {'col_0'}, dimensions={0}, use_global_device_ids=true | all-gather | bytes 2560 | tf_op jit(solution)/shard_map/all_gather | solution.py:15
  17.3 4.6 %all-gather.19 = f32[2,1,128]{2,1,0:T(1,128)S(1)} all-gather(f32[1,1,128]{2,1,0:T(1,128)S(1)} %bitcast.60), channel_id=6, replica_groups=mesh['row'=8,'col_0'=4,'col_1'=2,'col_2'=2] {'col_1'}, dimensions={0}, use_global_device_ids=true | all-gather | bytes 1536 | tf_op jit(solution)/shard_map/all_gather | solution.py:15
  21.9 5.3 %all-gather.20 = f32[2,1,128]{2,1,0:T(1,128)S(1)} all-gather(f32[1,1,128]{2,1,0:T(1,128)S(1)} %bitcast.61), channel_id=7, replica_groups=mesh['row'=8,'col_0'=4,'col_1'=2,'col_2'=2] {'col_2'}, dimensions={0}, use_global_device_ids=true | all-gather | bytes 1536 | tf_op jit(solution)/shard_map/all_gather | solution.py:15
  27.2 0.7 rsqrt_multiply_fusion.5
  27.9 0.7 fusion
  28.6 4.9 %all-to-all-start.1 = ((bf16[16,8,512]{2,1,0:T(8,128)(2,1)}), bf16[16,8,512]{2,1,0:T(8,128)(2,1)S(1)}, u32[]{:S(2)}, u32[]{:S(2)}) async-start(bf16[16,8,512]{2,1,0:T(8,128)(2,1)} %fusion), calls=%async_computation.1 | async-start | bytes 262144 | tf_op jit(solution)/shard_map/all_to_all | solution.py:30
  33.6 1.2 dynamic-slice
  35.5 6.4 %multiply_reduce_fusion.1 = (f32[3696]{0:T(1024)S(1)}, f32[3696,512]{1,0:T(8,128)}) fusion(bf16[3696,64]{0,1:T(8,128)(2,1)S(1)} %copy-done, bf16[64,512]{1,0:T(8,128)(2,1)} %param.41, bf16[3696,512]{1,0:T(8,128)(2,1)} %param.40), kind=kOutput, calls=%fused_computation.4 | convolution fusion | flops 249786768 | bytes 11907520 | tf_op jit(solution)/shard_map/dot_general | solution.py:21
  42.0 0.4 dynamic-update-slice
  42.5 6.5 %multiply_reduce_fusion = (f32[3696]{0:T(1024)S(1)}, f32[3696,512]{1,0:T(8,128)}) fusion(bf16[3696,64]{0,1:T(8,128)(2,1)S(1)} %copy-done.3, bf16[64,512]{1,0:T(8,128)(2,1)S(1)} %copy-done.9, bf16[3696,512]{1,0:T(8,128)(2,1)} %param.44), kind=kOutput, calls=%fused_computation.1 | convolution fusion | flops 249786768 | bytes 11907520 | tf_op jit(solution)/shard_map/dot_general | solution.py:21
  49.0 0.4 dynamic-update-slice.3
  49.4 0.6 copy-done.4
  50.1 1.3 copy.49
  51.4 1.7 multiply_reduce_fusion.2
  53.2 9.7 %all-gather.9 = f32[4096]{0:T(1024)S(1)} all-gather(f32[1024]{0:T(1024)S(1)} %get-tuple-element.18), channel_id=11, replica_groups=mesh['row'=8,'col_0'=4,'col_1'=2,'col_2'=2] {'col_0'}, dimensions={0}, use_global_device_ids=true | all-gather | bytes 20480 | tf_op jit(solution)/shard_map/all_gather | solution.py:15
  62.9 4.7 %all-gather.10 = f32[2048]{0:T(1024)S(1)} all-gather(f32[1024]{0:T(1024)S(1)} %reduce_sum.229), channel_id=12, replica_groups=mesh['row'=8,'col_0'=4,'col_1'=2,'col_2'=2] {'col_1'}, dimensions={0}, use_global_device_ids=true | all-gather | bytes 12288 | tf_op jit(solution)/shard_map/all_gather | solution.py:15
  67.7 5.9 %all-gather.11 = f32[2048]{0:T(1024)S(1)} all-gather(f32[1024]{0:T(1024)S(1)} %reduce_sum.230), channel_id=13, replica_groups=mesh['row'=8,'col_0'=4,'col_1'=2,'col_2'=2] {'col_2'}, dimensions={0}, use_global_device_ids=true | all-gather | bytes 12288 | tf_op jit(solution)/shard_map/all_gather | solution.py:15
  73.6 0.3 multiply_reduce_fusion.4
  73.9 7.2 %all-gather.21 = f32[4,1,128]{2,1,0:T(1,128)S(1)} all-gather(f32[1,1,128]{2,1,0:T(1,128)S(1)} %bitcast.59), channel_id=8, replica_groups=mesh['row'=8,'col_0'=4,'col_1'=2,'col_2'=2] {'col_0'}, dimensions={0}, use_global_device_ids=true | all-gather | bytes 2560 | tf_op jit(solution)/shard_map/all_gather | solution.py:15
  81.1 4.6 %all-gather.22 = f32[2,1,128]{2,1,0:T(1,128)S(1)} all-gather(f32[1,1,128]{2,1,0:T(1,128)S(1)} %bitcast.62), channel_id=9, replica_groups=mesh['row'=8,'col_0'=4,'col_1'=2,'col_2'=2] {'col_1'}, dimensions={0}, use_global_device_ids=true | all-gather | bytes 1536 | tf_op jit(solution)/shard_map/all_gather | solution.py:15
  85.7 5.0 %all-gather.23 = f32[2,1,128]{2,1,0:T(1,128)S(1)} all-gather(f32[1,1,128]{2,1,0:T(1,128)S(1)} %bitcast.63), channel_id=10, replica_groups=mesh['row'=8,'col_0'=4,'col_1'=2,'col_2'=2] {'col_2'}, dimensions={0}, use_global_device_ids=true | all-gather | bytes 1536 | tf_op jit(solution)/shard_map/all_gather | solution.py:15
  90.7 0.7 fusion.1
  91.5 4.9 %all-to-all-start.2 = ((bf16[16,8,512]{2,1,0:T(8,128)(2,1)}), bf16[16,8,512]{2,1,0:T(8,128)(2,1)S(1)}, u32[]{:S(2)}, u32[]{:S(2)}) async-start(bf16[16,8,512]{2,1,0:T(8,128)(2,1)} %fusion.1), calls=%async_computation.2 | async-start | bytes 262144 | tf_op jit(solution)/shard_map/all_to_all | solution.py:30
  96.4 1.2 multiply_convert_fusion.2
  97.7 6.4 %all-to-all-done.2 = bf16[16,8,512]{2,1,0:T(8,128)(2,1)S(1)} async-done(((bf16[16,8,512]{2,1,0:T(8,128)(2,1)}), bf16[16,8,512]{2,1,0:T(8,128)(2,1)S(1)}, u32[]{:S(2)}, u32[]{:S(2)}) %all-to-all-start.2) | async-done | bytes 131104 | tf_op jit(solution)/shard_map/all_to_all | solution.py:30
  104.0 5.1 %all-to-all-start.3 = ((bf16[1024,8,64]{0,2,1:T(8,128)(2,1)}), bf16[1024,8,64]{0,2,1:T(8,128)(2,1)}, u32[]{:S(2)}, u32[]{:S(2)}) async-start(bf16[1024,8,64]{0,2,1:T(8,128)(2,1)} %bitcast.49), calls=%async_computation.3 | async-start | bytes 2097152 | tf_op jit(solution)/shard_map/all_to_all | solution.py:63
  109.2 1.8 multiply_reduce_fusion.3
  110.9 10.1 %all-gather = f32[4096]{0:T(1024)S(1)} all-gather(f32[1024]{0:T(1024)S(1)} %get-tuple-element.12), channel_id=2, replica_groups=mesh['row'=8,'col_0'=4,'col_1'=2,'col_2'=2] {'col_0'}, dimensions={0}, use_global_device_ids=true | all-gather | bytes 20480 | tf_op jit(solution)/shard_map/all_gather | solution.py:15
  121.1 4.7 %all-gather.1 = f32[2048]{0:T(1024)S(1)} all-gather(f32[1024]{0:T(1024)S(1)} %reduce_sum.217), channel_id=3, replica_groups=mesh['row'=8,'col_0'=4,'col_1'=2,'col_2'=2] {'col_1'}, dimensions={0}, use_global_device_ids=true | all-gather | bytes 12288 | tf_op jit(solution)/shard_map/all_gather | solution.py:15
  125.8 5.5 %all-gather.2 = f32[2048]{0:T(1024)S(1)} all-gather(f32[1024]{0:T(1024)S(1)} %reduce_sum.218), channel_id=4, replica_groups=mesh['row'=8,'col_0'=4,'col_1'=2,'col_2'=2] {'col_2'}, dimensions={0}, use_global_device_ids=true | all-gather | bytes 12288 | tf_op jit(solution)/shard_map/all_gather | solution.py:15
  131.3 1.2 multiply_convert_fusion.3
  132.5 0.6 dynamic-slice.1
  133.8 0.6 dynamic-slice.2
  135.0 0.9 reshape.48
  136.0 0.9 reshape.51
  137.0 0.4 dynamic-update-slice.1
  137.4 0.4 dynamic-update-slice.4
  137.8 7.8 %all-reduce.8 = (f32[7392]{0:T(1024)S(1)}, f32[7392]{0:T(1024)S(1)}) all-reduce(f32[7392]{0:T(1024)S(1)} %dynamic-update-slice.1, f32[7392]{0:T(1024)S(1)} %dynamic-update-slice.4), channel_id=15, replica_groups=mesh['row'=8,'col_0'=4,'col_1'=2,'col_2'=2] {'col_1'}, use_global_device_ids=true, to_apply=%add.1 | all-reduce | flops 14784 | bytes 118272
  145.6 0.1 reshape.52
  145.7 0.1 reshape.49
  145.9 0.4 dynamic-update-slice.5
  146.3 0.4 dynamic-update-slice.2
  146.7 5.9 %all-reduce.7 = (f32[7392]{0:T(1024)S(1)}, f32[7392]{0:T(1024)S(1)}) all-reduce(f32[7392]{0:T(1024)S(1)} %dynamic-update-slice.2, f32[7392]{0:T(1024)S(1)} %dynamic-update-slice.5), channel_id=16, replica_groups=mesh['row'=8,'col_0'=4,'col_1'=2,'col_2'=2] {'col_2'}, use_global_device_ids=true, to_apply=%add.2 | all-reduce | flops 14784 | bytes 118272
  152.7 4.9 %all-to-all-start = ((bf16[16,64,512]{2,1,0:T(8,128)(2,1)}), bf16[16,64,512]{2,1,0:T(8,128)(2,1)S(1)}, u32[]{:S(2)}, u32[]{:S(2)}) async-start(bf16[16,64,512]{2,1,0:T(8,128)(2,1)} %bitcast.50), calls=%async_computation | async-start | bytes 2097152 | tf_op jit(solution)/shard_map/all_to_all | solution.py:30
  157.7 5.3 %multiply_convert_fusion = bf16[3696,512]{1,0:T(8,128)(2,1)} fusion(f32[3696,512]{1,0:T(8,128)} %get-tuple-element.23, f32[3696]{0:T(1024)S(1)} %rsqrt_multiply_fusion), kind=kLoop, calls=%fused_computation | loop fusion | flops 3784704 | bytes 11368896 | tf_op jit(solution)/shard_map/convert_element_type | solution.py:25
  163.0 4.0 %all_to_all.104 = bf16[16,231,512]{2,1,0:T(8,128)(2,1)} reshape(bf16[3696,512]{1,0:T(8,128)(2,1)} %multiply_convert_fusion) | data formatting | bytes 7569408 | tf_op jit(solution)/shard_map/all_to_all | solution.py:30
  166.9 7.8 %all-to-all-done = bf16[16,64,512]{2,1,0:T(8,128)(2,1)S(1)} async-done(((bf16[16,64,512]{2,1,0:T(8,128)(2,1)}), bf16[16,64,512]{2,1,0:T(8,128)(2,1)S(1)}, u32[]{:S(2)}, u32[]{:S(2)}) %all-to-all-start) | async-done | bytes 1048608 | tf_op jit(solution)/shard_map/all_to_all | solution.py:30
  174.8 5.3 %all-to-all-start.5 = ((bf16[16,231,512]{2,1,0:T(8,128)(2,1)}), bf16[16,231,512]{2,1,0:T(8,128)(2,1)}, u32[]{:S(2)}, u32[]{:S(2)}) async-start(bf16[16,231,512]{2,1,0:T(8,128)(2,1)} %all_to_all.104), calls=%async_computation.5 | async-start | bytes 7602176 | tf_op jit(solution)/shard_map/all_to_all | solution.py:30
  180.2 5.3 %multiply_convert_fusion.1 = bf16[3696,512]{1,0:T(8,128)(2,1)} fusion(f32[3696,512]{1,0:T(8,128)} %get-tuple-element.21, f32[3696]{0:T(1024)S(1)} %rsqrt_multiply_fusion.1), kind=kLoop, calls=%fused_computation.3 | loop fusion | flops 3784704 | bytes 11368896 | tf_op jit(solution)/shard_map/convert_element_type | solution.py:25
  185.5 4.0 %all_to_all.100 = bf16[16,231,512]{2,1,0:T(8,128)(2,1)} reshape(bf16[3696,512]{1,0:T(8,128)(2,1)} %multiply_convert_fusion.1) | data formatting | bytes 7569408 | tf_op jit(solution)/shard_map/all_to_all | solution.py:30
  189.5 37.4 %all-to-all-done.5 = bf16[16,231,512]{2,1,0:T(8,128)(2,1)} async-done(((bf16[16,231,512]{2,1,0:T(8,128)(2,1)}), bf16[16,231,512]{2,1,0:T(8,128)(2,1)}, u32[]{:S(2)}, u32[]{:S(2)}) %all-to-all-start.5) | async-done | bytes 3784736 | tf_op jit(solution)/shard_map/all_to_all | solution.py:30
  226.8 5.3 %all-to-all-start.4 = ((bf16[16,231,512]{2,1,0:T(8,128)(2,1)}), bf16[16,231,512]{2,1,0:T(8,128)(2,1)}, u32[]{:S(2)}, u32[]{:S(2)}) async-start(bf16[16,231,512]{2,1,0:T(8,128)(2,1)} %all_to_all.100), calls=%async_computation.4 | async-start | bytes 7602176 | tf_op jit(solution)/shard_map/all_to_all | solution.py:30
  232.1 2.3 copy.54
  234.4 1.1 copy.53
  235.5 3.4 %copy.52 = bf16[231,16,512]{2,1,0:T(8,128)(2,1)S(1)} copy(bf16[231,16,512]{2,0,1:T(8,128)(2,1)} %bitcast.20) | data formatting | bytes 7569408 | tf_op jit(solution)/shard_map/all_to_all | solution.py:30
  238.8 0.4 pad.1
  239.2 5.8 %copy.56 = bf16[29,8,16,512]{3,1,2,0:T(8,128)(2,1)} copy(bf16[29,8,16,512]{3,2,1,0:T(8,128)(2,1)S(1)} %bitcast.48) | data formatting | bytes 7602176
  245.0 33.9 %all-to-all-done.4 = bf16[16,231,512]{2,1,0:T(8,128)(2,1)} async-done(((bf16[16,231,512]{2,1,0:T(8,128)(2,1)}), bf16[16,231,512]{2,1,0:T(8,128)(2,1)}, u32[]{:S(2)}, u32[]{:S(2)}) %all-to-all-start.4) | async-done | bytes 3784736 | tf_op jit(solution)/shard_map/all_to_all | solution.py:30
  278.9 3.4 %copy.51 = bf16[231,16,512]{2,1,0:T(8,128)(2,1)S(1)} copy(bf16[231,16,512]{2,0,1:T(8,128)(2,1)} %bitcast.19) | data formatting | bytes 7569408 | tf_op jit(solution)/shard_map/all_to_all | solution.py:30
  282.3 0.4 pad
  282.7 5.8 %copy.55 = bf16[29,8,16,512]{3,1,2,0:T(8,128)(2,1)} copy(bf16[29,8,16,512]{3,2,1,0:T(8,128)(2,1)S(1)} %bitcast.47) | data formatting | bytes 7602176
  288.5 0.7 copy.85
  289.1 0.7 copy.86
  (83 shorter events, 1.0 us)
Async XLA Ops:
  7.2 28.3 %copy-start = (bf16[3696,64]{0,1:T(8,128)(2,1)S(1)}, bf16[3696,64]{0,1:T(8,128)(2,1)}, u32[]{:S(2)}) copy-start(bf16[3696,64]{0,1:T(8,128)(2,1)} %param.42) | copy-start | bytes 1419268
  28.6 62.9 %all-to-all-start.1 = ((bf16[16,8,512]{2,1,0:T(8,128)(2,1)}), bf16[16,8,512]{2,1,0:T(8,128)(2,1)S(1)}, u32[]{:S(2)}, u32[]{:S(2)}) async-start(bf16[16,8,512]{2,1,0:T(8,128)(2,1)} %fusion), calls=%async_computation.1 | async-start | bytes 262144 | tf_op jit(solution)/shard_map/all_to_all | solution.py:30
  33.6 101.5 %all-reduce.11.cloned.1.call-start = ((), (), s32[]{:S(2)}) async-start(), calls=%async_computation.6 | async-start | bytes 245760
  35.5 6.9 %copy-start.3 = (bf16[3696,64]{0,1:T(8,128)(2,1)S(1)}, bf16[3696,64]{0,1:T(8,128)(2,1)}, u32[]{:S(2)}) copy-start(bf16[3696,64]{0,1:T(8,128)(2,1)} %param.46) | copy-start | bytes 1419268
  35.5 6.9 %copy-start.9 = (bf16[64,512]{1,0:T(8,128)(2,1)S(1)}, bf16[64,512]{1,0:T(8,128)(2,1)}, u32[]{:S(2)}) copy-start(bf16[64,512]{1,0:T(8,128)(2,1)} %param.45) | copy-start | bytes 196612
  42.4 6.6 %copy-start.5 = (f32[14784]{0:T(1024)}, f32[14784]{0:T(1024)S(1)}, u32[]{:S(2)}) copy-start(f32[14784]{0:T(1024)S(1)} %dynamic-update-slice) | copy-start | bytes 177412
  42.4 7.7 %copy-start.2 = (bf16[1024,512]{1,0:T(8,128)(2,1)S(1)}, bf16[1024,512]{1,0:T(8,128)(2,1)}, u32[]{:S(2)}) copy-start(bf16[1024,512]{1,0:T(8,128)(2,1)} %param.36) | copy-start | bytes 3145732
  42.4 9.0 %copy-start.6 = (bf16[1024,64]{0,1:T(8,128)(2,1)S(1)}, bf16[1024,64]{0,1:T(8,128)(2,1)}, u32[]{:S(2)}) copy-start(bf16[1024,64]{0,1:T(8,128)(2,1)} %param.38) | copy-start | bytes 393220
  42.4 9.0 %copy-start.10 = (bf16[64,512]{1,0:T(8,128)(2,1)S(1)}, bf16[64,512]{1,0:T(8,128)(2,1)}, u32[]{:S(2)}) copy-start(bf16[64,512]{1,0:T(8,128)(2,1)} %param.37) | copy-start | bytes 196612
  49.0 24.6 %copy-start.7 = (bf16[128,512]{1,0:T(8,128)(2,1)S(1)}, bf16[128,512]{1,0:T(8,128)(2,1)}, u32[]{:S(2)}) copy-start(bf16[128,512]{1,0:T(8,128)(2,1)} %param.32) | copy-start | bytes 393220
  49.0 24.6 %copy-start.12 = (bf16[64,512]{1,0:T(8,128)(2,1)S(1)}, bf16[64,512]{1,0:T(8,128)(2,1)}, u32[]{:S(2)}) copy-start(bf16[64,512]{1,0:T(8,128)(2,1)} %param.33) | copy-start | bytes 196612
  49.0 24.6 %copy-start.13 = (bf16[128,64]{0,1:T(8,128)(2,1)S(1)}, bf16[128,64]{0,1:T(8,128)(2,1)}, u32[]{:S(2)}) copy-start(bf16[128,64]{0,1:T(8,128)(2,1)} %param.34) | copy-start | bytes 49156
  49.0 41.8 %copy-start.18 = (f32[128]{0:T(128)S(1)}, f32[128]{0:T(128)}, u32[]{:S(2)}) copy-start(f32[128]{0:T(128)} %param.35) | copy-start | bytes 1540
  49.0 42.5 %copy-start.16 = (f32[1024]{0:T(1024)S(1)}, f32[1024]{0:T(1024)}, u32[]{:S(2)}) copy-start(f32[1024]{0:T(1024)} %param.39) | copy-start | bytes 12292
  49.4 0.6 copy-start.4
  53.1 56.0 %copy-start.8 = (bf16[1024,64]{0,1:T(8,128)(2,1)S(1)}, bf16[1024,64]{0,1:T(8,128)(2,1)}, u32[]{:S(2)}) copy-start(bf16[1024,64]{0,1:T(8,128)(2,1)} %param.26) | copy-start | bytes 393220
  53.1 56.0 %copy-start.11 = (bf16[64,512]{1,0:T(8,128)(2,1)S(1)}, bf16[64,512]{1,0:T(8,128)(2,1)}, u32[]{:S(2)}) copy-start(bf16[64,512]{1,0:T(8,128)(2,1)} %param.25) | copy-start | bytes 196612
  91.5 12.5 %all-to-all-start.2 = ((bf16[16,8,512]{2,1,0:T(8,128)(2,1)}), bf16[16,8,512]{2,1,0:T(8,128)(2,1)S(1)}, u32[]{:S(2)}, u32[]{:S(2)}) async-start(bf16[16,8,512]{2,1,0:T(8,128)(2,1)} %fusion.1), calls=%async_computation.2 | async-start | bytes 262144 | tf_op jit(solution)/shard_map/all_to_all | solution.py:30
  96.4 34.9 %copy-start.17 = (f32[1024]{0:T(1024)S(1)}, f32[1024]{0:T(1024)}, u32[]{:S(2)}) copy-start(f32[1024]{0:T(1024)} %param.27) | copy-start | bytes 12292
  104.0 48.7 %all-to-all-start.3 = ((bf16[1024,8,64]{0,2,1:T(8,128)(2,1)}), bf16[1024,8,64]{0,2,1:T(8,128)(2,1)}, u32[]{:S(2)}, u32[]{:S(2)}) async-start(bf16[1024,8,64]{0,2,1:T(8,128)(2,1)} %bitcast.49), calls=%async_computation.3 | async-start | bytes 2097152 | tf_op jit(solution)/shard_map/all_to_all | solution.py:63
  109.1 23.4 %copy-start.20 = (u32[128]{0:T(128)S(1)}, u32[128]{0:T(128)}, u32[]{:S(2)}) copy-start(u32[128]{0:T(128)} %constant.13) | copy-start | bytes 1540
  109.1 24.6 %copy-start.19 = (u32[128]{0:T(128)S(1)}, u32[128]{0:T(128)}, u32[]{:S(2)}) copy-start(u32[128]{0:T(128)} %constant.18) | copy-start | bytes 1540
  109.1 43.6 %copy-start.14 = (f32[3696]{0:T(1024)S(1)}, f32[3696]{0:T(1024)}, u32[]{:S(2)}) copy-start(f32[3696]{0:T(1024)} %param.47) | copy-start | bytes 44356
  152.7 22.0 %all-to-all-start = ((bf16[16,64,512]{2,1,0:T(8,128)(2,1)}), bf16[16,64,512]{2,1,0:T(8,128)(2,1)S(1)}, u32[]{:S(2)}, u32[]{:S(2)}) async-start(bf16[16,64,512]{2,1,0:T(8,128)(2,1)} %bitcast.50), calls=%async_computation | async-start | bytes 2097152 | tf_op jit(solution)/shard_map/all_to_all | solution.py:30
  166.9 13.3 %copy-start.15 = (f32[3696]{0:T(1024)S(1)}, f32[3696]{0:T(1024)}, u32[]{:S(2)}) copy-start(f32[3696]{0:T(1024)} %param.43) | copy-start | bytes 44356
  174.8 52.1 %all-to-all-start.5 = ((bf16[16,231,512]{2,1,0:T(8,128)(2,1)}), bf16[16,231,512]{2,1,0:T(8,128)(2,1)}, u32[]{:S(2)}, u32[]{:S(2)}) async-start(bf16[16,231,512]{2,1,0:T(8,128)(2,1)} %all_to_all.104), calls=%async_computation.5 | async-start | bytes 7602176 | tf_op jit(solution)/shard_map/all_to_all | solution.py:30
  226.8 52.1 %all-to-all-start.4 = ((bf16[16,231,512]{2,1,0:T(8,128)(2,1)}), bf16[16,231,512]{2,1,0:T(8,128)(2,1)}, u32[]{:S(2)}, u32[]{:S(2)}) async-start(bf16[16,231,512]{2,1,0:T(8,128)(2,1)} %all_to_all.100), calls=%async_computation.4 | async-start | bytes 7602176 | tf_op jit(solution)/shard_map/all_to_all | solution.py:30
  282.7 7.1 %copy-start.1 = (bf16[3696,64]{0,1:T(8,128)(2,1)S(1)}, bf16[3696,64]{0,1:T(8,128)(2,1)}, u32[]{:S(2)}) copy-start(bf16[3696,64]{0,1:T(8,128)(2,1)} %param.42) | copy-start | bytes 1419268
Sparse Core Ops, SparseCore 0:
  50.2 41.3 all-reduce.10
